TPU v7x, 256 devices: a whole 4x4x8 slice. The times are simulated.
256 devices in a mesh: grp: 8 (over y, core), head: 32 (over z, x).
Axes of the slice: x: 4, y: 4, z: 8, core: 2. Of those that a mesh axis runs over, the one named last changes fastest.
Arguments:
- hidden_in: bfloat16 [192, 4096], P('grp', 'head'), may hold values from -6 to 6
- attention_gain: float32 [4096], replicated, may hold values from 0.1 to 1.9
- w_query: bfloat16 [4096, 4096], P(None, 'head'), may hold values from -0.09375 to 0.09375
- w_key_value: bfloat16 [2, 4096, 4096], P(None, None, 'head'), as said below
- w_attention_out: bfloat16 [4096, 4096], P('head'), may hold values from -0.09375 to 0.09375
- past_cache: bfloat16 [2, 192, 32, 128, 128], P(None, 'grp', 'head'), may hold values from -2000 to 2000, as said below
- lengths: int32 [192], P('grp'), may hold values from 2 to 128, as said below
- mamba_gain: float32 [4096], replicated, may hold values from 0.1 to 1.9
- w_in: bfloat16 [2, 4096, 8192], P(None, None, 'head'), may hold values from -0.09375 to 0.09375
- filter_weight: float32 [4, 8192], P(None, 'head'), may hold values from -3 to 3
- filter_bias: float32 [8192], P('head'), may hold values from -1.8 to 1.8
- filter_state: float32 [192, 3, 8192], P('grp', None, 'head'), may hold values from -6 to 6
- w_select: bfloat16 [8192, 288], P('head'), may hold values from -0.0625 to 0.0625
- w_step: bfloat16 [256, 8192], P(None, 'head'), may hold values from -0.375 to 0.375
- step_bias: float32 [8192], P('head'), may hold values from -4 to -1
- log_rate: float32 [16, 8192], P(None, 'head'), may hold values from 0 to 2.77
- skip_gain: float32 [8192], P('head'), may hold values from 0.1 to 1.9
- scan_state: float32 [192, 16, 8192], P('grp', None, 'head'), may hold values from -6 to 6
- w_mamba_out: bfloat16 [8192, 4096], P('head'), may hold values from -0.0625 to 0.0625
- reward_terms: float32 [192, 128], P('grp', 'head'), may hold values from -60 to 60
- reward_mask: int32 [192, 128], P('grp', 'head'), may hold values 0 or 1
Outputs:
- hidden_out: bfloat16 [192, 4096], P('grp', 'head')
- new_key_value: bfloat16 [2, 192, 32, 128], P(None, 'grp', 'head')
- new_filter_state: float32 [192, 3, 8192], P('grp', None, 'head')
- new_scan_state: float32 [192, 16, 8192], P('grp', None, 'head')
- rewards: float32 [192], P('grp')
Inputs may be any that keep to these rules, and one draw needn't show every extreme that they name: `w_key_value`: query heads that share a key-value head (4 of them in a row) hold equal copies. `past_cache`: query heads that share a key-value head (4 of them in a row) hold equal copies. `lengths`: the first sample's cache is full (128).
All inputs are finite; a program needn't handle non-finite values. No bound on the sum of `reward_mask` on one device may be relied on, other than what follows from the above.
Results may differ from a plain program's by a relative error of at most 0.012.
Values may be sent and summed in bfloat16 or wider, within the bound.
A program may use at most 64 MiB of HBM per device.

v0:
```python
import math

import jax
import jax.numpy as jnp
from jax import lax
from jax.sharding import PartitionSpec as P

EPS = 1e-06


def joined_along(pieces, dim):
    pieces = jnp.moveaxis(pieces, 0, dim)
    shape = pieces.shape
    return pieces.reshape(*shape[:dim], shape[dim] * shape[dim + 1], *shape[dim + 2 :])


def from_everyone(value, axis):
    size = lax.axis_size(axis)
    return lax.all_to_all(
        jnp.broadcast_to(value[None], (size, *value.shape)), axis, 0, 0, tiled=True
    )


def gathered_copies(value, axis, dim):
    return joined_along(from_everyone(value, axis), dim)


def in_blocks(value, dim, size):
    before, after = (value.shape[:dim], value.shape[dim + 1 :])
    return jnp.moveaxis(value.reshape(*before, size, -1, *after), dim, 0)


def summed_on_arrival(value, axis, dim):
    pieces = in_blocks(value, dim, lax.axis_size(axis))
    arrived = lax.all_to_all(pieces, axis, split_axis=0, concat_axis=0, tiled=True)
    return arrived.sum(axis=0)


def of_everyone(value, axis):
    everything = from_everyone(value, axis)
    return jnp.sum(everything, axis=0)


def packed_total(arrays, axis):
    ends = [0]
    for a in arrays:
        ends.append(ends[-1] + a.size)
    running = of_everyone(jnp.concatenate([a.ravel() for a in arrays]), axis)
    return tuple((running[b:e].reshape(a.shape) for a, b, e in zip(arrays, ends, ends[1:])))


def norm_rows(row_values, gain):
    values = row_values.astype(jnp.float32)
    factor = lax.rsqrt(jnp.mean(values * values, axis=-1, keepdims=True) + EPS)
    return (values * factor * gain).astype(jnp.bfloat16)


def attend_block(queries, past_cache, fresh, lengths):
    inv_root = 1.0 / math.sqrt(queries.shape[-1])
    scores = (
        jnp.einsum("bhd,bhtd->bht", queries, past_cache[0], preferred_element_type=jnp.float32)
        * inv_root
    )
    positions = lax.iota(jnp.int32, past_cache.shape[3])
    scores = jnp.where(positions[None, None, :] < lengths[:, None, None], scores, -jnp.inf)
    own_score = (
        jnp.einsum("bhd,bhd->bh", queries, fresh[0], preferred_element_type=jnp.float32) * inv_root
    )
    row_max = jnp.maximum(jnp.max(scores, axis=-1), own_score)
    weights = jnp.exp(scores - row_max[:, :, None])
    own_weight = jnp.exp(own_score - row_max)
    denominator = jnp.sum(weights, axis=-1) + own_weight
    weights = (weights / denominator[:, :, None]).astype(jnp.bfloat16)
    own_weight = (own_weight / denominator).astype(jnp.bfloat16)
    blended = jnp.einsum(
        "bht,bhtd->bhd", weights, past_cache[1], preferred_element_type=jnp.float32
    )
    blended = blended + own_weight.astype(jnp.float32)[:, :, None] * fresh[1].astype(jnp.float32)
    return blended.astype(jnp.bfloat16)


def reward_partial(reward_terms, reward_mask, lengths):
    columns = reward_terms.shape[1]
    positions = lax.axis_index("head") * columns + lax.iota(jnp.int32, columns)
    live = (reward_mask == 1) & (positions[None, :] < lengths[:, None])
    return jnp.sum(jnp.where(live, reward_terms, 0.0), axis=1)


def local(
    hidden_in,
    attention_gain,
    w_query,
    w_key_value,
    w_attention_out,
    past_cache,
    lengths,
    mamba_gain,
    w_in,
    filter_weight,
    filter_bias,
    filter_state,
    w_select,
    w_step,
    step_bias,
    log_rate,
    skip_gain,
    scan_state,
    w_mamba_out,
    reward_terms,
    reward_mask,
):
    samples = hidden_in.shape[0]
    local_heads = past_cache.shape[2]
    head_size = past_cache.shape[4]
    rank_width = w_step.shape[0]
    state_width = log_rate.shape[0]
    full_in = gathered_copies(hidden_in, "head", 1)
    normed = norm_rows(full_in, attention_gain)
    queries = jnp.dot(normed, w_query, preferred_element_type=jnp.float32).astype(jnp.bfloat16)
    queries = queries.reshape(samples, local_heads, head_size)
    fresh_all = jnp.einsum("bd,kdc->kbc", normed, w_key_value, preferred_element_type=jnp.float32)
    new_key_value = fresh_all.astype(jnp.bfloat16).reshape(2, samples, local_heads, head_size)
    attended = attend_block(queries, past_cache, new_key_value, lengths)
    attended = attended.reshape(samples, local_heads * head_size)
    head_terms = jnp.dot(attended, w_attention_out, preferred_element_type=jnp.float32)
    summed = summed_on_arrival(head_terms, "head", 1)
    mixed = (hidden_in.astype(jnp.float32) + summed).astype(jnp.bfloat16)
    mixed_full = gathered_copies(mixed, "head", 1)
    normed_two = norm_rows(mixed_full, mamba_gain)
    x_inner = jnp.dot(normed_two, w_in[0], preferred_element_type=jnp.float32)
    gate_part = jnp.dot(normed_two, w_in[1], preferred_element_type=jnp.float32)
    taps = filter_weight.shape[0]
    conv_sum = filter_bias + x_inner * filter_weight[taps - 1]
    for tap_index in range(taps - 1):
        conv_sum = conv_sum + filter_state[:, tap_index, :] * filter_weight[tap_index]
    conv_out = jax.nn.silu(conv_sum).astype(jnp.bfloat16)
    new_filter_state = jnp.concatenate([filter_state[:, 1:, :], x_inner[:, None, :]], axis=1)
    local_select = jnp.dot(conv_out, w_select, preferred_element_type=jnp.float32)
    projected, rewards = packed_total(
        (local_select, reward_partial(reward_terms, reward_mask, lengths)), "head"
    )
    step_low = projected[:, :rank_width].astype(jnp.bfloat16)
    b_input = projected[:, rank_width : rank_width + state_width]
    c_output = projected[:, rank_width + state_width :]
    step_size = jax.nn.softplus(
        jnp.dot(step_low, w_step, preferred_element_type=jnp.float32) + step_bias
    )
    conv_value = conv_out.astype(jnp.float32)
    decay_rate = jnp.exp(-step_size[:, None, :] * jnp.exp(log_rate)[None, :, :])
    new_scan_state = (
        decay_rate * scan_state
        + step_size[:, None, :] * b_input[:, :, None] * conv_value[:, None, :]
    )
    scan_out = (
        jnp.sum(c_output[:, :, None] * new_scan_state, axis=1) + skip_gain * conv_value
    ) * jax.nn.silu(gate_part)
    scan_out = scan_out.astype(jnp.bfloat16)
    channel_terms = jnp.dot(scan_out, w_mamba_out, preferred_element_type=jnp.float32)
    mamba_sum = summed_on_arrival(channel_terms, "head", 1)
    hidden_out = (mixed.astype(jnp.float32) + mamba_sum).astype(jnp.bfloat16)
    return (hidden_out, new_key_value, new_filter_state, new_scan_state, rewards)


def solution(mesh):
    placed = (
        P("grp", "head"),
        P(),
        P(None, "head"),
        P(None, None, "head"),
        P("head", None),
        P(None, "grp", "head", None, None),
        P("grp"),
        P(),
        P(None, None, "head"),
        P(None, "head"),
        P("head"),
        P("grp", None, "head"),
        P("head", None),
        P(None, "head"),
        P("head"),
        P(None, "head"),
        P("head"),
        P("grp", None, "head"),
        P("head", None),
        P("grp", "head"),
        P("grp", "head"),
    )
    return jax.shard_map(
        local,
        mesh=mesh,
        in_specs=placed,
        out_specs=(
            P("grp", "head"),
            P(None, "grp", "head", None),
            P("grp", None, "head"),
            P("grp", None, "head"),
            P("grp"),
        ),
        check_vma=False,
    )
```

profile of v0, /device:TPU:8, one launch (start us, length us, event | category | flops | bytes accessed | tf_op | source)
XLA Modules:
  0.0 121.6 jit_solution(4849652033355117548)
XLA Ops:
  0.7 1.5 %broadcast_in_dim.15 = bf16[32,24,128]{2,1,0:T(8,128)(2,1)} broadcast(bf16[24,128]{1,0:T(8,128)(2,1)} %param.21), dimensions={1,2} | broadcast | bytes 202752 | tf_op jit(solution)/shard_map/broadcast_in_dim | solution.py:20
  2.2 11.3 %all-to-all-start = ((bf16[32,24,128]{2,1,0:T(8,128)(2,1)}), bf16[32,24,128]{2,1,0:T(8,128)(2,1)S(1)}, u32[]{:S(2)}, u32[]{:S(2)}) async-start(bf16[32,24,128]{2,1,0:T(8,128)(2,1)} %broadcast_in_dim.15), calls=%async_computation | async-start | bytes 393216 | tf_op jit(solution)/shard_map/all_to_all | solution.py:19
  13.5 1.6 %copy.58 = bf16[4096,128]{1,0:T(8,128)(2,1)S(1)} copy(bf16[4096,128]{0,1:T(8,128)(2,1)} %bitcast.136) | data formatting | bytes 2097152 | tf_op jit(solution)/shard_map/dot_general | solution.py:125
  15.2 10.0 %all-to-all-done = bf16[32,24,128]{2,1,0:T(8,128)(2,1)S(1)} async-done(((bf16[32,24,128]{2,1,0:T(8,128)(2,1)}), bf16[32,24,128]{2,1,0:T(8,128)(2,1)S(1)}, u32[]{:S(2)}, u32[]{:S(2)}) %all-to-all-start) | async-done | bytes 196640 | tf_op jit(solution)/shard_map/all_to_all | solution.py:19
  25.4 2.2 %convolution_convert_fusion = bf16[24,2,128]{2,0,1:T(8,128)(2,1)S(1)} fusion(bf16[2,4096,128]{2,1,0:T(8,128)(2,1)} %param.24, f32[4096]{0:T(1024)S(1)} %copy-done.5, f32[24]{0:T(128)S(1)} %add_rsqrt_fusion.1, bf16[32,24,128]{2,1,0:T(8,128)(2,1)S(1)} %all-to-all-done), kind=kOutput, calls=%fused_computation.9 | convolution fusion | flops 50731008 | bytes 2322528 | tf_op jit(solution)/shard_map/bd,kdc->kbc/dot_general | solution.py:121
  29.4 1.4 %convolution_bitcast_fusion.1 = f32[32,24,128]{2,1,0:T(8,128)} fusion(bf16[32,128,128]{2,1,0:T(8,128)(2,1)S(1)} %bitcast.135, f32[24,128]{1,0:T(8,128)S(1)} %bitcast.147, bf16[2,24,128]{2,1,0:T(8,128)(2,1)S(1)} %bitcast.142, f32[24]{0:T(128)S(1)} %get-tuple-element.45), kind=kOutput, calls=%fused_computation.7 | convolution fusion | flops 25178112 | bytes 1460736 | tf_op jit(solution)/shard_map/dot_general | solution.py:125
  30.8 3.9 %all-to-all-start.1 = ((f32[32,24,128]{2,1,0:T(8,128)}), f32[32,24,128]{2,1,0:T(8,128)S(1)}, u32[]{:S(2)}, u32[]{:S(2)}) async-start(f32[32,24,128]{2,1,0:T(8,128)} %convolution_bitcast_fusion.1), calls=%async_computation.1 | async-start | bytes 786432 | tf_op jit(solution)/shard_map/all_to_all | solution.py:35
  34.7 14.3 %all-to-all-done.1 = f32[32,24,128]{2,1,0:T(8,128)S(1)} async-done(((f32[32,24,128]{2,1,0:T(8,128)}), f32[32,24,128]{2,1,0:T(8,128)S(1)}, u32[]{:S(2)}, u32[]{:S(2)}) %all-to-all-start.1) | async-done | bytes 393248 | tf_op jit(solution)/shard_map/all_to_all | solution.py:35
  49.1 0.7 broadcast_in_dim.17
  49.8 4.3 %all-to-all-start.2 = ((bf16[32,24,128]{2,1,0:T(8,128)(2,1)}), bf16[32,24,128]{2,1,0:T(8,128)(2,1)S(1)}, u32[]{:S(2)}, u32[]{:S(2)}) async-start(bf16[32,24,128]{2,1,0:T(8,128)(2,1)} %broadcast_in_dim.17), calls=%async_computation.2 | async-start | bytes 393216 | tf_op jit(solution)/shard_map/all_to_all | solution.py:19
  54.3 11.0 %all-to-all-done.2 = bf16[32,24,128]{2,1,0:T(8,128)(2,1)S(1)} async-done(((bf16[32,24,128]{2,1,0:T(8,128)(2,1)}), bf16[32,24,128]{2,1,0:T(8,128)(2,1)S(1)}, u32[]{:S(2)}, u32[]{:S(2)}) %all-to-all-start.2) | async-done | bytes 196640 | tf_op jit(solution)/shard_map/all_to_all | solution.py:19
  65.5 2.1 %fusion.55 = (f32[24,256]{1,0:T(8,128)S(1)}, bf16[24,256]{1,0:T(8,128)(2,1)S(1)}, f32[24,256]{1,0:T(8,128)S(1)}) fusion(f32[256]{0:T(256)S(1)} %bitcast.151, f32[24,3,256]{2,0,1:T(8,128)S(1)} %copy-done.2, f32[256]{0:T(256)S(1)} %bitcast.152, f32[256]{0:T(256)S(1)} %bitcast.150, f32[256]{0:T(256)S(1)} %bitcast.149, f32[256]{0:T(256)S(1)} %copy-done.17, ...), kind=kOutput, calls=%fused_computation.83 | convolution fusion | flops 50810880 | bytes 2450528 | tf_op jit(solution)/shard_map/dot_general | solution.py:130
  67.9 1.4 %broadcast_in_dim.19 = f32[32,1,6936]{2,1,0:T(1,128)} broadcast(f32[6936]{0:T(1024)S(1)} %pad_maximum_fusion.1), dimensions={2} | broadcast | bytes 915552 | tf_op jit(solution)/shard_map/broadcast_in_dim | solution.py:20
  69.3 4.0 %all-to-all-start.3 = ((f32[32,1,6936]{2,1,0:T(1,128)}), f32[32,1,6936]{2,1,0:T(1,128)S(1)}, u32[]{:S(2)}, u32[]{:S(2)}) async-start(f32[32,1,6936]{2,1,0:T(1,128)} %broadcast_in_dim.19), calls=%async_computation.3 | async-start | bytes 1802240 | tf_op jit(solution)/shard_map/all_to_all | solution.py:19
  73.4 23.0 %all-to-all-done.3 = f32[32,1,6936]{2,1,0:T(1,128)S(1)} async-done(((f32[32,1,6936]{2,1,0:T(1,128)}), f32[32,1,6936]{2,1,0:T(1,128)S(1)}, u32[]{:S(2)}, u32[]{:S(2)}) %all-to-all-start.3) | async-done | bytes 887840 | tf_op jit(solution)/shard_map/all_to_all | solution.py:19
  96.4 0.5 reduce_sum.77
  97.3 1.9 %multiply_reduce_fusion = (f32[24,256]{1,0:T(8,128)S(1)}, f32[24,16,256]{2,1,0:T(8,128)}) fusion(f32[24,16]{1,0:T(8,128)S(1)} %get-tuple-element.40, f32[24,256]{1,0:T(8,128)S(1)} %get-tuple-element.37, f32[24,16]{1,0:T(8,128)S(1)} %get-tuple-element.39, f32[24,256]{1,0:T(8,128)S(1)} %get-tuple-element.51, f32[24,16,256]{2,1,0:T(8,128)} %param.38, ...), kind=kLoop, calls=%fused_computation.29 | loop fusion | flops 681984 | bytes 904192 | tf_op jit(solution)/shard_map/reduce_sum | solution.py:155
  99.2 2.9 %convolution_bitcast_fusion = f32[3,32,8,128]{3,2,1,0:T(8,128)S(1)} fusion(bf16[256,4096]{1,0:T(8,128)(2,1)S(1)} %copy-done, bf16[2,4096,256]{2,1,0:T(8,128)(2,1)} %param.29, f32[24,256]{1,0:T(8,128)S(1)} %get-tuple-element.35, f32[256]{0:T(256)S(1)} %copy-done.15, bf16[24,256]{1,0:T(8,128)(2,1)S(1)} %get-tuple-element.38, ...), kind=kOutput, calls=%fused_computation.6 | convolution fusion | flops 101111808 | bytes 4838496 | tf_op jit(solution)/shard_map/dot_general | solution.py:158
  102.1 0.8 copy.91
  102.9 5.1 %all-to-all-start.4 = ((f32[32,24,128]{2,1,0:T(8,128)}), f32[32,24,128]{2,1,0:T(8,128)S(1)}, u32[]{:S(2)}, u32[]{:S(2)}) async-start(f32[32,24,128]{2,1,0:T(8,128)} %bitcast.133), calls=%async_computation.4 | async-start | bytes 786432 | tf_op jit(solution)/shard_map/all_to_all | solution.py:35
  108.0 0.6 pad_maximum_fusion
  108.6 0.5 slice.85
  109.1 11.8 %all-to-all-done.4 = f32[32,24,128]{2,1,0:T(8,128)S(1)} async-done(((f32[32,24,128]{2,1,0:T(8,128)}), f32[32,24,128]{2,1,0:T(8,128)S(1)}, u32[]{:S(2)}, u32[]{:S(2)}) %all-to-all-start.4) | async-done | bytes 393248 | tf_op jit(solution)/shard_map/all_to_all | solution.py:35
  121.0 0.6 add_convert_fusion
  (63 shorter events, 3.0 us)
Async XLA Ops:
  0.6 98.6 %copy-start = (bf16[256,4096]{1,0:T(8,128)(2,1)S(1)}, bf16[256,4096]{1,0:T(8,128)(2,1)}, u32[]{:S(2)}) copy-start(bf16[256,4096]{1,0:T(8,128)(2,1)} %param.39) | copy-start | bytes 6291460
  0.6 24.7 %copy-start.5 = (f32[4096]{0:T(1024)S(1)}, f32[4096]{0:T(1024)}, u32[]{:S(2)}) copy-start(f32[4096]{0:T(1024)} %param.22) | copy-start | bytes 49156
  2.2 23.0 %all-to-all-start = ((bf16[32,24,128]{2,1,0:T(8,128)(2,1)}), bf16[32,24,128]{2,1,0:T(8,128)(2,1)S(1)}, u32[]{:S(2)}, u32[]{:S(2)}) async-start(bf16[32,24,128]{2,1,0:T(8,128)(2,1)} %broadcast_in_dim.15), calls=%async_computation | async-start | bytes 393216 | tf_op jit(solution)/shard_map/all_to_all | solution.py:19
  25.2 2.4 %copy-start.1 = (bf16[4096,128]{1,0:T(8,128)(2,1)S(1)}, bf16[4096,128]{1,0:T(8,128)(2,1)}, u32[]{:S(2)}) copy-start(bf16[4096,128]{1,0:T(8,128)(2,1)} %param.23) | copy-start | bytes 3145732
  25.2 2.8 %copy-start.16 = (bf16[2,24,1,128,128]{4,3,2,1,0:T(8,128)(2,1)S(1)}, bf16[2,24,1,128,128]{4,3,2,1,0:T(8,128)(2,1)}, u32[]{:S(2)}) copy-start(bf16[2,24,1,128,128]{4,3,2,1,0:T(8,128)(2,1)} %param.26) | copy-start | bytes 4718596
  25.4 3.2 %copy-start.10 = (s32[24]{0:T(128)S(1)}, s32[24]{0:T(128)}, u32[]{:S(2)}) copy-start(s32[24]{0:T(128)} %param.27) | copy-start | bytes 292
  27.5 3.3 %copy-start.6 = (bf16[24,2,128]{2,0,1:T(8,128)(2,1)}, bf16[24,2,128]{2,0,1:T(8,128)(2,1)S(1)}, u32[]{:S(2)}) copy-start(bf16[24,2,128]{2,0,1:T(8,128)(2,1)S(1)} %convolution_convert_fusion) | copy-start | bytes 36868
  28.0 21.1 %copy-start.7 = (bf16[24,128]{1,0:T(8,128)(2,1)S(1)}, bf16[24,128]{1,0:T(8,128)(2,1)}, u32[]{:S(2)}) copy-start(bf16[24,128]{1,0:T(8,128)(2,1)} %param.21) | copy-start | bytes 18436
  28.5 25.6 %copy-start.12 = (f32[24,4]{0,1:T(4,128)S(1)}, f32[24,4]{0,1:T(4,128)}, u32[]{:S(2)}) copy-start(f32[24,4]{0,1:T(4,128)} %param.40) | copy-start | bytes 1156
  28.5 25.6 %copy-start.13 = (s32[24,4]{0,1:T(4,128)S(1)}, s32[24,4]{0,1:T(4,128)}, u32[]{:S(2)}) copy-start(s32[24,4]{0,1:T(4,128)} %param.41) | copy-start | bytes 1156
  28.5 25.7 %copy-start.11 = (f32[4,256]{1,0:T(4,128)S(1)}, f32[4,256]{1,0:T(4,128)}, u32[]{:S(2)}) copy-start(f32[4,256]{1,0:T(4,128)} %param.30) | copy-start | bytes 12292
  29.0 36.4 %copy-start.2 = (f32[24,3,256]{2,0,1:T(8,128)S(1)}, f32[24,3,256]{2,0,1:T(8,128)}, u32[]{:S(2)}) copy-start(f32[24,3,256]{2,0,1:T(8,128)} %param.32) | copy-start | bytes 221188
  29.1 36.4 %copy-start.8 = (f32[4096]{0:T(1024)S(1)}, f32[4096]{0:T(1024)}, u32[]{:S(2)}) copy-start(f32[4096]{0:T(1024)} %param.28) | copy-start | bytes 49156
  29.1 36.4 %copy-start.17 = (f32[256]{0:T(256)S(1)}, f32[256]{0:T(256)}, u32[]{:S(2)}) copy-start(f32[256]{0:T(256)} %param.31) | copy-start | bytes 3076
  30.8 18.2 %all-to-all-start.1 = ((f32[32,24,128]{2,1,0:T(8,128)}), f32[32,24,128]{2,1,0:T(8,128)S(1)}, u32[]{:S(2)}, u32[]{:S(2)}) async-start(f32[32,24,128]{2,1,0:T(8,128)} %convolution_bitcast_fusion.1), calls=%async_computation.1 | async-start | bytes 786432 | tf_op jit(solution)/shard_map/all_to_all | solution.py:35
  34.7 32.9 %copy-start.3 = (bf16[256,288]{0,1:T(8,128)(2,1)S(1)}, bf16[256,288]{0,1:T(8,128)(2,1)}, u32[]{:S(2)}) copy-start(bf16[256,288]{0,1:T(8,128)(2,1)} %param.33) | copy-start | bytes 442372
  49.8 15.5 %all-to-all-start.2 = ((bf16[32,24,128]{2,1,0:T(8,128)(2,1)}), bf16[32,24,128]{2,1,0:T(8,128)(2,1)S(1)}, u32[]{:S(2)}, u32[]{:S(2)}) async-start(bf16[32,24,128]{2,1,0:T(8,128)(2,1)} %broadcast_in_dim.17), calls=%async_computation.2 | async-start | bytes 393216 | tf_op jit(solution)/shard_map/all_to_all | solution.py:19
  67.5 5.8 %copy-start.9 = (f32[16,256]{1,0:T(8,128)S(1)}, f32[16,256]{1,0:T(8,128)}, u32[]{:S(2)}) copy-start(f32[16,256]{1,0:T(8,128)} %param.36) | copy-start | bytes 49156
  67.6 29.5 %copy-start.4 = (bf16[256,256]{1,0:T(8,128)(2,1)S(1)}, bf16[256,256]{1,0:T(8,128)(2,1)}, u32[]{:S(2)}) copy-start(bf16[256,256]{1,0:T(8,128)(2,1)} %param.34) | copy-start | bytes 393220
  67.6 29.5 %copy-start.14 = (f32[256]{0:T(256)S(1)}, f32[256]{0:T(256)}, u32[]{:S(2)}) copy-start(f32[256]{0:T(256)} %param.35) | copy-start | bytes 3076
  69.3 29.9 %copy-start.15 = (f32[256]{0:T(256)S(1)}, f32[256]{0:T(256)}, u32[]{:S(2)}) copy-start(f32[256]{0:T(256)} %param.37) | copy-start | bytes 3076
  69.3 27.1 %all-to-all-start.3 = ((f32[32,1,6936]{2,1,0:T(1,128)}), f32[32,1,6936]{2,1,0:T(1,128)S(1)}, u32[]{:S(2)}, u32[]{:S(2)}) async-start(f32[32,1,6936]{2,1,0:T(1,128)} %broadcast_in_dim.19), calls=%async_computation.3 | async-start | bytes 1802240 | tf_op jit(solution)/shard_map/all_to_all | solution.py:19
  99.2 8.8 %slice-start = ((f32[24,3,256]{2,0,1:T(8,128)}), f32[24,2,256]{2,0,1:T(8,128)S(1)}, s32[]{:S(2)}) async-start(f32[24,3,256]{2,0,1:T(8,128)} %param.32), calls=%async_computation.5 | async-start | bytes 98304 | tf_op jit(solution)/shard_map/slice | solution.py:137
  102.9 18.1 %all-to-all-start.4 = ((f32[32,24,128]{2,1,0:T(8,128)}), f32[32,24,128]{2,1,0:T(8,128)S(1)}, u32[]{:S(2)}, u32[]{:S(2)}) async-start(f32[32,24,128]{2,1,0:T(8,128)} %bitcast.133), calls=%async_computation.4 | async-start | bytes 786432 | tf_op jit(solution)/shard_map/all_to_all | solution.py:35
where the time goes:
time: 122 us
  waiting for transfers between devices  70.2 us (58%)
  starting transfers between devices  28.6 us (23%)
  matrix products  10.1 us (8%)
  local copies, waits for them, and re-layouts  6.99 us (6%)
  other arithmetic  4.7 us (4%)
    all_to_all x3, waiting for transfers between devices, from_everyone(): lax.all_to_all(jnp.broadcast_to(value[None], (size, *value.shape)), axis,...  44 us
    all_to_all x2, waiting for transfers between devices, summed_on_arrival(): lax.all_to_all(pieces, axis, split_axis=0, concat_axis=0, tiled=True)  26.2 us
    all_to_all x3, starting transfers between devices, from_everyone(): lax.all_to_all(jnp.broadcast_to(value[None], (size, *value.shape)), axis,...  19.7 us
    all_to_all x2, starting transfers between devices, summed_on_arrival(): lax.all_to_all(pieces, axis, split_axis=0, concat_axis=0, tiled=True)  8.93 us
    broadcast_in_dim x3, local copies, waits for them, and re-layouts, from_everyone(): jnp.broadcast_to(value[None], (size, *value.shape))  3.66 us
    dot_general x1, matrix products, local(): jnp.dot(scan_out, w_mamba_out, preferred_element_type=jnp.float32)  2.93 us
  transfers between devices with their start and end apart: 5, of which 5 were waited for; matrix products, arithmetic and copies ran while one was open for 2% of the time, Pallas kernels for 0%

commit v1 on v0

v1 whole, which is shorter than its diff:
```python
import math

import jax
import jax.numpy as jnp
from jax import lax
from jax.experimental import pallas as pl
from jax.experimental.pallas import tpu as pltpu
from jax.sharding import PartitionSpec as P

EPS = 1e-06
BF16 = jnp.bfloat16
F32 = jnp.float32
Z_SIZE = 8
X_SIZE = 4


def outward(step, half):
    return half + ((step + 1) // 2) * (1 - 2 * (step % 2))


def step_kernel(
    hidden_hbm,
    gain_one_hbm,
    w_query_hbm,
    w_kv_hbm,
    w_out_hbm,
    cache_hbm,
    lengths_hbm,
    gain_two_hbm,
    w_in_hbm,
    taps_hbm,
    tap_bias_hbm,
    filter_hbm,
    w_select_hbm,
    w_step_hbm,
    step_bias_hbm,
    rate_hbm,
    skip_hbm,
    state_hbm,
    w_mamba_hbm,
    terms_hbm,
    mask_hbm,
    hidden_out,
    kv_out,
    filter_out,
    state_out,
    rewards_out,
    hidden,
    gain_one,
    w_qkv,
    w_out,
    keys,
    values,
    lengths,
    gain_two,
    w_in,
    taps,
    tap_bias,
    filters,
    w_select,
    w_step,
    step_bias,
    rate,
    skip,
    state,
    w_mamba,
    terms,
    mask,
    gathered,
    send_heads,
    got_heads,
    mixed,
    gathered_two,
    send_x,
    got_x,
    send_z,
    got_z,
    send_channels,
    got_channels,
    load_sems,
    send_sems,
    recv_sems,
):
    samples, width = hidden.shape
    heads = gathered.shape[0]
    channels = w_step.shape[1]
    rank = w_step.shape[0]
    n_state = rate.shape[0]
    me = lax.axis_index("head")
    z = me // X_SIZE
    x = me % X_SIZE

    def any_peer(i):
        dz = outward(i // X_SIZE, Z_SIZE // 2)
        dx = outward(i % X_SIZE, X_SIZE // 2)
        return ((z + dz) % Z_SIZE) * X_SIZE + (x + dx) % X_SIZE

    def x_peer(i):
        return z * X_SIZE + (x + outward(i, X_SIZE // 2)) % X_SIZE

    def z_peer(i):
        return ((z + outward(i, Z_SIZE // 2)) % Z_SIZE) * X_SIZE + x

    barrier = pltpu.get_barrier_semaphore()

    def greet(i, carry):
        pl.semaphore_signal(
            barrier, inc=1, device_id={"head": any_peer(i)}, device_id_type=pl.DeviceIdType.MESH
        )
        return carry

    lax.fori_loop(0, heads - 1, greet, 0)

    loads = []

    def load(source, target):
        copy = pltpu.make_async_copy(source, target, load_sems.at[len(loads)])
        copy.start()
        loads.append(copy)
        return copy

    load_hidden = [load(hidden_hbm, hidden), load(hidden_hbm, gathered.at[me])]
    load_qkv = [
        load(gain_one_hbm, gain_one),
        load(w_query_hbm, w_qkv.at[:, 0:width]),
        load(w_kv_hbm.at[0], w_qkv.at[:, width : 2 * width]),
        load(w_kv_hbm.at[1], w_qkv.at[:, 2 * width : 3 * width]),
    ]
    load_cache = [
        load(cache_hbm.at[0], keys),
        load(cache_hbm.at[1], values),
        load(lengths_hbm, lengths),
        load(w_out_hbm, w_out),
        load(terms_hbm, terms),
        load(mask_hbm, mask),
    ]
    load_in = [
        load(gain_two_hbm, gain_two),
        load(w_in_hbm, w_in),
        load(taps_hbm, taps),
        load(tap_bias_hbm, tap_bias),
        load(filter_hbm, filters),
        load(w_select_hbm, w_select),
    ]
    load_scan = [
        load(w_step_hbm, w_step),
        load(step_bias_hbm, step_bias),
        load(rate_hbm, rate),
        load(skip_hbm, skip),
        load(state_hbm, state),
        load(w_mamba_hbm, w_mamba),
    ]

    def wait_all(copies):
        for copy in copies:
            copy.wait()

    def send(phase, source, target, peer, count):
        def one(i, carry):
            to = peer(i)
            pltpu.make_async_remote_copy(
                src_ref=source(to),
                dst_ref=target,
                send_sem=send_sems.at[phase],
                recv_sem=recv_sems.at[phase],
                device_id={"head": to},
                device_id_type=pl.DeviceIdType.MESH,
            ).start()
            return carry

        lax.fori_loop(0, count, one, 0)

    def bytes_of(phase, buffer, count):
        part = buffer.at[pl.ds(0, count)]
        return pltpu.make_async_remote_copy(
            src_ref=part,
            dst_ref=part,
            send_sem=send_sems.at[phase],
            recv_sem=recv_sems.at[phase],
            device_id={"head": me},
            device_id_type=pl.DeviceIdType.MESH,
        )

    def normed_rows(blocks, gains):
        wide = [blocks[h].astype(F32) for h in range(heads)]
        squares = wide[0] * wide[0]
        for block in wide[1:]:
            squares = squares + block * block
        mean = jnp.sum(squares, axis=1, keepdims=True) * (1.0 / (heads * width))
        factor = lax.rsqrt(mean + EPS)
        return jnp.concatenate(
            [(wide[h] * factor * gains[h : h + 1, :]).astype(BF16) for h in range(heads)], axis=1
        )

    def summed(blocks, count):
        total = blocks[0].astype(F32)
        for h in range(1, count):
            total = total + blocks[h].astype(F32)
        return total

    wait_all(load_hidden)
    pl.semaphore_wait(barrier, heads - 1)
    send(0, lambda to: hidden, gathered.at[me], any_peer, heads - 1)
    wait_all(load_qkv)
    wait_all(load_cache)

    lane = lax.broadcasted_iota(jnp.int32, (samples, width), 1)
    row = lax.broadcasted_iota(jnp.int32, (samples, width), 0)

    def as_column(line):
        wide = jnp.concatenate([line, jnp.zeros((1, width - samples), F32)], axis=1)
        return jnp.sum(jnp.where(lane == row, wide, 0.0), axis=1, keepdims=True)

    length = as_column(lengths[...].astype(F32))
    own_columns = terms.shape[0]
    position = lax.broadcasted_iota(jnp.int32, terms.shape, 0) + me * own_columns
    live = (mask[...] == 1) & (position < lengths[...])
    reward_part = as_column(
        jnp.sum(jnp.where(live, terms[...], 0.0), axis=0, keepdims=True)
    )

    bytes_of(0, gathered, heads - 1).wait_recv()

    normed = normed_rows(gathered, gain_one)
    qkv = jnp.dot(normed, w_qkv[...], preferred_element_type=F32).astype(BF16)
    query = qkv[:, 0:width]
    new_key = qkv[:, width : 2 * width]
    new_value = qkv[:, 2 * width : 3 * width]
    kv_out[0] = new_key
    kv_out[1] = new_value
    inv_root = 1.0 / math.sqrt(width)
    context = keys.shape[0] // samples
    products = lax.dot_general(
        query, keys[...], (((1,), (1,)), ((), ())), preferred_element_type=F32
    )
    scores = products[:, 0:context]
    for b in range(1, samples):
        scores = jnp.where(row == b, products[:, b * context : (b + 1) * context], scores)
    scores = jnp.where(lane.astype(F32) < length, scores * inv_root, -jnp.inf)
    own = (
        jnp.sum(query.astype(F32) * new_key.astype(F32), axis=1, keepdims=True) * inv_root
    )
    top = jnp.maximum(jnp.max(scores, axis=1, keepdims=True), own)
    weights = jnp.exp(scores - top)
    own_weight = jnp.exp(own - top)
    total = jnp.sum(weights, axis=1, keepdims=True) + own_weight
    weights = weights / total
    own_weight = (own_weight / total).astype(BF16).astype(F32)
    placed = jnp.concatenate(
        [jnp.where(row == b, weights, 0.0).astype(BF16) for b in range(samples)], axis=1
    )
    blended = jnp.dot(placed, values[...], preferred_element_type=F32)
    attended = (blended + own_weight * new_value.astype(F32)).astype(BF16)

    head_terms = jnp.dot(attended, w_out[...], preferred_element_type=F32).astype(BF16)
    for h in range(heads):
        send_heads[h] = head_terms[:, h * width : (h + 1) * width]
    send(1, lambda to: send_heads.at[to], got_heads.at[me], any_peer, heads - 1)
    got_heads[me] = send_heads[me]
    wait_all(load_in)
    filter_sum = tap_bias[...] + filters[0] * taps[0:1, :]
    n_taps = taps.shape[0]
    for k in range(1, n_taps - 1):
        filter_sum = filter_sum + filters[k] * taps[k : k + 1, :]
    bytes_of(1, got_heads, heads - 1).wait_recv()
    mixed_block = (hidden[...].astype(F32) + summed(got_heads, heads)).astype(BF16)
    mixed[...] = mixed_block

    gathered_two[me] = mixed_block
    send(2, lambda to: mixed, gathered_two.at[me], any_peer, heads - 1)
    wait_all(load_scan)
    decay = jnp.exp(rate[...])
    bytes_of(2, gathered_two, heads - 1).wait_recv()

    normed_two = normed_rows(gathered_two, gain_two)
    x_inner = jnp.dot(normed_two, w_in[0], preferred_element_type=F32)
    conv_sum = filter_sum + x_inner * taps[n_taps - 1 : n_taps, :]
    conv_out = (conv_sum * jax.nn.sigmoid(conv_sum)).astype(BF16)
    across = (((1,), (1,)), ((), ()))
    select_low = lax.dot_general(
        conv_out, w_select[0:rank, :], across, preferred_element_type=F32
    )
    select_maps = lax.dot_general(
        conv_out, w_select[rank:, :], across, preferred_element_type=F32
    )
    n_maps = 2 * n_state
    half = width // 2

    def with_rest(block):
        high = block.astype(BF16)
        rest = block - high.astype(F32)
        return (high.astype(F32) + pltpu.roll(rest, half, 1)).astype(BF16)

    extra = jnp.concatenate(
        [select_maps, reward_part, jnp.zeros((samples, width - n_maps - 1), F32)], axis=1
    )
    packed = jnp.concatenate([select_low.astype(BF16), with_rest(extra)], axis=1)
    send_x[...] = packed
    got_x[x] = packed
    send(3, lambda to: send_x, got_x.at[x], x_peer, X_SIZE - 1)
    gate_part = jnp.dot(normed_two, w_in[1], preferred_element_type=F32)
    gate = gate_part * jax.nn.sigmoid(gate_part)
    bytes_of(3, got_x, X_SIZE - 1).wait_recv()

    def joined(total):
        low = total[:, 0:rank]
        rest = total[:, rank:]
        return low, jnp.where(lane < half, rest + pltpu.roll(rest, half, 1), 0.0)

    low, extra = joined(summed(got_x, X_SIZE))
    packed = jnp.concatenate([low.astype(BF16), with_rest(extra)], axis=1)
    send_z[...] = packed
    got_z[z] = packed
    send(4, lambda to: send_z, got_z.at[z], z_peer, Z_SIZE - 1)
    for k in range(n_taps - 2):
        filter_out[k] = filters[k + 1]
    filter_out[n_taps - 2] = x_inner
    conv_value = conv_out.astype(F32)
    skipped = skip[...] * conv_value
    bytes_of(4, got_z, Z_SIZE - 1).wait_recv()
    low, extra = joined(summed(got_z, Z_SIZE))

    pre_step = jnp.dot(low.astype(BF16), w_step[...], preferred_element_type=F32) + step_bias[...]
    step_size = jnp.maximum(pre_step, 0.0) + jnp.log1p(jnp.exp(-jnp.abs(pre_step)))
    driven = step_size * conv_value
    turned = jnp.transpose(
        jnp.concatenate([extra, jnp.zeros((width - samples, width), F32)], axis=0)
    )
    rewards_out[...] = turned[n_maps : n_maps + 1, 0:samples]
    scanned = []
    for b in range(samples):
        new_state = (
            jnp.exp(-step_size[b : b + 1, :] * decay) * state[b]
            + turned[0:n_state, b : b + 1] * driven[b : b + 1, :]
        )
        state_out[b] = new_state
        scanned.append(
            jnp.sum(turned[n_state:n_maps, b : b + 1] * new_state, axis=0, keepdims=True)
        )
    scan_out = ((jnp.concatenate(scanned, axis=0) + skipped) * gate).astype(BF16)

    channel_terms = jnp.dot(scan_out, w_mamba[...], preferred_element_type=F32).astype(BF16)
    for h in range(heads):
        send_channels[h] = channel_terms[:, h * width : (h + 1) * width]
    send(5, lambda to: send_channels.at[to], got_channels.at[me], any_peer, heads - 1)
    got_channels[me] = send_channels[me]
    for phase, buffer, count in (
        (0, gathered, heads - 1),
        (1, got_heads, heads - 1),
        (2, gathered_two, heads - 1),
        (3, got_x, X_SIZE - 1),
        (4, got_z, Z_SIZE - 1),
    ):
        bytes_of(phase, buffer, count).wait_send()
    bytes_of(5, got_channels, heads - 1).wait_recv()
    hidden_out[...] = (mixed[...].astype(F32) + summed(got_channels, heads)).astype(BF16)
    bytes_of(5, got_channels, heads - 1).wait_send()


def write_kernel(*refs):
    sems = refs[-1]
    count = (len(refs) - 1) // 2
    copies = [
        pltpu.make_async_copy(refs[i], refs[count + i], sems.at[i]) for i in range(count)
    ]
    for copy in copies:
        copy.start()
    for copy in copies:
        copy.wait()


def local(
    hidden_in,
    attention_gain,
    w_query,
    w_key_value,
    w_attention_out,
    past_cache,
    lengths,
    mamba_gain,
    w_in,
    filter_weight,
    filter_bias,
    filter_state,
    w_select,
    w_step,
    step_bias,
    log_rate,
    skip_gain,
    scan_state,
    w_mamba_out,
    reward_terms,
    reward_mask,
):
    samples, width = hidden_in.shape
    features = w_query.shape[0]
    heads = features // width
    context, head_size = past_cache.shape[3:]
    channels = w_step.shape[1]
    rank = w_step.shape[0]
    select = w_select.shape[1]
    n_taps = filter_weight.shape[0]
    n_state = log_rate.shape[0]
    lanes = -(-select // width) * width
    operands = (
        hidden_in,
        attention_gain.reshape(heads, width),
        w_query,
        w_key_value,
        w_attention_out,
        past_cache.reshape(2, samples * context, head_size),
        lengths.reshape(1, samples),
        mamba_gain.reshape(heads, width),
        w_in,
        filter_weight,
        filter_bias.reshape(1, channels),
        jnp.swapaxes(filter_state, 0, 1),
        w_select.T,
        w_step,
        step_bias.reshape(1, channels),
        log_rate,
        skip_gain.reshape(1, channels),
        scan_state,
        w_mamba_out,
        reward_terms.T,
        reward_mask.T,
    )
    scratch = [
        pltpu.VMEM((samples, width), BF16),
        pltpu.VMEM((heads, width), F32),
        pltpu.VMEM((features, 3 * width), BF16),
        pltpu.VMEM((width, features), BF16),
        pltpu.VMEM((samples * context, head_size), BF16),
        pltpu.VMEM((samples * context, head_size), BF16),
        pltpu.VMEM((1, samples), jnp.int32),
        pltpu.VMEM((heads, width), F32),
        pltpu.VMEM(w_in.shape, BF16),
        pltpu.VMEM(filter_weight.shape, F32),
        pltpu.VMEM((1, channels), F32),
        pltpu.VMEM((n_taps - 1, samples, channels), F32),
        pltpu.VMEM((select, channels), BF16),
        pltpu.VMEM(w_step.shape, BF16),
        pltpu.VMEM((1, channels), F32),
        pltpu.VMEM(log_rate.shape, F32),
        pltpu.VMEM((1, channels), F32),
        pltpu.VMEM(scan_state.shape, F32),
        pltpu.VMEM(w_mamba_out.shape, BF16),
        pltpu.VMEM(reward_terms.shape[::-1], F32),
        pltpu.VMEM(reward_mask.shape[::-1], jnp.int32),
        pltpu.VMEM((heads, samples, width), BF16),
        pltpu.VMEM((heads, samples, width), BF16),
        pltpu.VMEM((heads, samples, width), BF16),
        pltpu.VMEM((samples, width), BF16),
        pltpu.VMEM((heads, samples, width), BF16),
        pltpu.VMEM((samples, lanes), BF16),
        pltpu.VMEM((X_SIZE, samples, lanes), BF16),
        pltpu.VMEM((samples, lanes), BF16),
        pltpu.VMEM((Z_SIZE, samples, lanes), BF16),
        pltpu.VMEM((heads, samples, width), BF16),
        pltpu.VMEM((heads, samples, width), BF16),
        pltpu.SemaphoreType.DMA((24,)),
        pltpu.SemaphoreType.DMA((6,)),
        pltpu.SemaphoreType.DMA((6,)),
    ]
    vmem = pl.BlockSpec(memory_space=pltpu.VMEM)
    hbm = pl.BlockSpec(memory_space=pltpu.HBM)
    results = (
        ((samples, width), BF16),
        ((2, samples, width), BF16),
        ((n_taps - 1, samples, channels), F32),
        (scan_state.shape, F32),
        ((1, samples), F32),
    )
    found = pl.pallas_call(
        step_kernel,
        out_shape=tuple(pltpu.VMEM(shape, dtype) for shape, dtype in results),
        in_specs=[hbm] * len(operands),
        out_specs=[vmem] * len(results),
        scratch_shapes=scratch,
        compiler_params=pltpu.CompilerParams(
            collective_id=0, has_side_effects=True, vmem_limit_bytes=40 * 1024 * 1024
        ),
        name="decode_step",
    )(*(pltpu.with_memory_space_constraint(a, pltpu.HBM) for a in operands))
    hidden_out, new_kv, new_filter, new_state, rewards = pl.pallas_call(
        write_kernel,
        out_shape=tuple(pltpu.HBM(shape, dtype) for shape, dtype in results),
        in_specs=[vmem] * len(results),
        out_specs=[hbm] * len(results),
        scratch_shapes=[pltpu.SemaphoreType.DMA((len(results),))],
        compiler_params=pltpu.CompilerParams(vmem_limit_bytes=16 * 1024 * 1024),
        name="write_results",
    )(*(pltpu.with_memory_space_constraint(a, pltpu.VMEM) for a in found))
    return (
        hidden_out,
        new_kv.reshape(2, samples, 1, width),
        jnp.swapaxes(new_filter, 0, 1),
        new_state,
        rewards.reshape(samples),
    )


def solution(mesh):
    placed = (
        P("grp", "head"),
        P(),
        P(None, "head"),
        P(None, None, "head"),
        P("head", None),
        P(None, "grp", "head", None, None),
        P("grp"),
        P(),
        P(None, None, "head"),
        P(None, "head"),
        P("head"),
        P("grp", None, "head"),
        P("head", None),
        P(None, "head"),
        P("head"),
        P(None, "head"),
        P("head"),
        P("grp", None, "head"),
        P("head", None),
        P("grp", "head"),
        P("grp", "head"),
    )
    return jax.shard_map(
        local,
        mesh=mesh,
        in_specs=placed,
        out_specs=(
            P("grp", "head"),
            P(None, "grp", "head", None),
            P("grp", None, "head"),
            P("grp", None, "head"),
            P("grp"),
        ),
        check_vma=False,
    )
```

time: 122 us -> 51.1 us (0.42)
  waiting for transfers between devices: 70.2 us -> 0 us
  Pallas kernels: 0 us -> 50.3 us
  starting transfers between devices: 28.6 us -> 0 us
  matrix products: 10.1 us -> 0 us
  local copies, waits for them, and re-layouts: 6.99 us -> 0 us
  other arithmetic: 4.7 us -> 0 us
    all_to_all x5 -> x0, waiting for transfers between devices: 70.2 us -> none  [the longest x3 44 us: from_everyone(): lax.all_to_all(jnp.broadcast_to(value[None], (size, *value.shape)), axis,...]
    pallas_call x0 -> x2, Pallas kernels: none -> 50.3 us  [the longest x1 49.4 us: local(): pl.pallas_call(step_kernel, out_shape=tuple((pltpu.VMEM(shape, dtype) for...]
    all_to_all x5 -> x0, starting transfers between devices: 28.6 us -> none  [the longest x3 19.7 us: from_everyone(): lax.all_to_all(jnp.broadcast_to(value[None], (size, *value.shape)), axis,...]
    dot_general x9 -> x0, matrix products: 10.1 us -> none  [the longest x1 2.93 us: local(): jnp.dot(scan_out, w_mamba_out, preferred_element_type=jnp.float32)]
    broadcast_in_dim x3 -> x0, local copies, waits for them, and re-layouts: 3.66 us -> none  [from_everyone(): jnp.broadcast_to(value[None], (size, *value.shape))]
    reduce_sum x8 -> x0, other arithmetic: 3.13 us -> none  [the longest x1 1.92 us: local(): jnp.sum(c_output[:, :, None] * new_scan_state, axis=1)]
    dot_general x1 -> x0, local copies, waits for them, and re-layouts: 1.62 us -> none  [local(): jnp.dot(attended, w_attention_out, preferred_element_type=jnp.float32)]
  transfers between devices with their start and end apart: 5 -> 0, of which waited for: 5 -> 0; matrix products, arithmetic and copies ran while one was open for 2% -> 0% of each run, Pallas kernels for 0% -> 0%
where the time goes in v1:
time: 51.1 us; the launch traced here: 50.9 us
  Pallas kernels  50.3 us (98%)
  between operations  0.65 us (1%)
    pallas_call x1, Pallas kernels, local(): pl.pallas_call(step_kernel, out_shape=tuple((pltpu.VMEM(shape, dtype) for...  49.4 us

profile of v1, /device:TPU:8, one launch (start us, length us, event | category | flops | bytes accessed | tf_op | source)
XLA Modules:
  0.0 50.9 jit_solution(560603560117235621)
XLA Ops:
  0.6 49.4 %decode_step.1 = (bf16[24,128]{1,0:T(8,128)(2,1)S(1)}, bf16[2,24,128]{2,1,0:T(8,128)(2,1)S(1)}, f32[3,24,256]{2,1,0:T(8,128)S(1)}, f32[24,16,256]{2,1,0:T(8,128)S(1)}, f32[1,24]{1,0:T(1,128)S(1)}) custom-call(bf16[24,128]{1,0:T(8,128)(2,1)} %hidden_hbm.1, f32[32,128]{1,0:T(8,128)} %bitcast.19, bf16[4096,128]{1,0:T(8,128)(2,1)} %w_query_hbm.1, ...), custom_call_target="tpu_custom_call" | custom-call | tf_op jit(solution)/shard_map/decode_step/pallas_call | solution.py:474
  50.1 0.8 %write_results.1 = (bf16[24,128]{1,0:T(8,128)(2,1)}, bf16[2,24,128]{2,1,0:T(8,128)(2,1)}, f32[3,24,256]{2,1,0:T(8,128)}, f32[24,16,256]{2,1,0:T(8,128)}, f32[1,24]{1,0:T(1,128)}) custom-call(bf16[24,128]{1,0:T(8,128)(2,1)S(1)} %get-tuple-element.15.refs_0_, bf16[2,24,128]{2,1,0:T(8,128)(2,1)S(1)} %get-tuple-element.16.refs_1_, ...), custom_call_target="tpu_custom_call" | custom-call | tf_op jit(solution)/shard_map/write_results/pallas_call | solution.py:485

commit v2 on v1

--- a/solution.py
+++ b/solution.py
@@ -50,6 +50,7 @@
     w_qkv,
     w_out,
     keys,
+    keys_turned,
     values,
     lengths,
     gain_two,
@@ -78,6 +79,11 @@
     send_channels,
     got_channels,
     load_sems,
+    filtered,
+    arrived,
+    along_x,
+    along_z_sent,
+    along_z,
     send_sems,
     recv_sems,
 ):
@@ -90,26 +96,39 @@
     z = me // X_SIZE
     x = me % X_SIZE
 
-    def any_peer(i):
-        dz = outward(i // X_SIZE, Z_SIZE // 2)
-        dx = outward(i % X_SIZE, X_SIZE // 2)
-        return ((z + dz) % Z_SIZE) * X_SIZE + (x + dx) % X_SIZE
-
     def x_peer(i):
         return z * X_SIZE + (x + outward(i, X_SIZE // 2)) % X_SIZE
 
     def z_peer(i):
         return ((z + outward(i, Z_SIZE // 2)) % Z_SIZE) * X_SIZE + x
 
+    core = lax.axis_index("grp") % 2
     barrier = pltpu.get_barrier_semaphore()
 
-    def greet(i, carry):
-        pl.semaphore_signal(
-            barrier, inc=1, device_id={"head": any_peer(i)}, device_id_type=pl.DeviceIdType.MESH
-        )
-        return carry
-
-    lax.fori_loop(0, heads - 1, greet, 0)
+    ring_rows = (4, 3, 5, 2, 6, 1, 7, 0)
+
+    def row_start(dz):
+        return ((z + dz) % Z_SIZE) * X_SIZE
+
+    def in_row(dz):
+        return X_SIZE if dz else X_SIZE - 1
+
+    def hops(offset):
+        dz, dx = offset
+        return min(dz, Z_SIZE - dz) + min(dx, X_SIZE - dx)
+
+    def farthest_first(rows):
+        offsets = [(dz, dx) for dz in rows for dx in range(X_SIZE) if dz or dx]
+        return sorted(offsets, key=hops, reverse=True)
+
+    with jax.named_scope("greet"):
+        for dz, dx in farthest_first(ring_rows):
+            pl.semaphore_signal(
+                barrier,
+                inc=1,
+                device_id={"head": row_start(dz) + (x + dx) % X_SIZE},
+                device_id_type=pl.DeviceIdType.MESH,
+            )
 
     loads = []
 
@@ -155,7 +174,7 @@
         for copy in copies:
             copy.wait()
 
-    def send(phase, source, target, peer, count):
+    def send(phase, source, target, peer, first, last):
         def one(i, carry):
             to = peer(i)
             pltpu.make_async_remote_copy(
@@ -168,7 +187,7 @@
             ).start()
             return carry
 
-        lax.fori_loop(0, count, one, 0)
+        lax.fori_loop(first, last, one, 0)
 
     def bytes_of(phase, buffer, count):
         part = buffer.at[pl.ds(0, count)]
@@ -181,16 +200,116 @@
             device_id_type=pl.DeviceIdType.MESH,
         )
 
-    def normed_rows(blocks, gains):
-        wide = [blocks[h].astype(F32) for h in range(heads)]
-        squares = wide[0] * wide[0]
-        for block in wide[1:]:
-            squares = squares + block * block
+    def send_to(offset, sem, source, target):
+        dz, dx = offset
+        to = row_start(dz) + (x + dx) % X_SIZE
+        pltpu.make_async_remote_copy(
+            src_ref=source(to),
+            dst_ref=target,
+            send_sem=send_sems.at[sem],
+            recv_sem=recv_sems.at[sem],
+            device_id={"head": to},
+            device_id_type=pl.DeviceIdType.MESH,
+        ).start()
+
+    def gather(sem, source, target):
+        for offset in farthest_first(ring_rows):
+            send_to(offset, sem + offset[0], lambda to: source, target)
+
+    depth = X_SIZE * width
+
+    def row_at(first):
+        return pl.ds(pl.multiple_of(first * width, depth), depth)
+
+    def scaled_row(first, blocks, gains):
+        wide = [blocks[first + k].astype(F32) for k in range(X_SIZE)]
+        scale = gains[pl.ds(first, X_SIZE), :]
+        scaled = [(wide[k] * scale[k : k + 1, :]).astype(BF16) for k in range(X_SIZE)]
+        return wide, jnp.concatenate(scaled, axis=1)
+
+    def projected_rows(sem, blocks, gains, weights):
+        squares = jnp.zeros((samples, width), F32)
+        total = jnp.zeros((samples, weights(pl.ds(0, depth)).shape[1]), F32)
+        for dz in ring_rows:
+            first = row_start(Z_SIZE - dz)
+            with jax.named_scope("wait_row"):
+                bytes_of(sem + dz, blocks, in_row(dz)).wait_recv()
+            wide, scaled = scaled_row(first, blocks, gains)
+            for block in wide:
+                squares = squares + block * block
+            total = total + jnp.dot(
+                scaled, weights(row_at(first)), preferred_element_type=F32
+            )
+        return squares, total
+
+    def place_terms(rows, weights, sent, some_rows):
+        for dz in some_rows:
+            first = row_start(dz)
+            part = jnp.dot(
+                rows, weights[:, row_at(first)], preferred_element_type=F32
+            ).astype(BF16)
+            for k in range(X_SIZE):
+                sent[first // X_SIZE, k] = part[:, k * width : (k + 1) * width]
+
+    def scatter_sums(sem, rows, weights, sent, landed, result, meanwhile):
+        @pl.when(core == 0)
+        def _():
+            for half in (ring_rows[:4], ring_rows[4:]):
+                place_terms(rows, weights, sent, half)
+                for offset in farthest_first(half):
+                    send_to(
+                        offset,
+                        sem,
+                        lambda to: sent.at[to // X_SIZE, to % X_SIZE],
+                        landed.at[me],
+                    )
+            landed[me] = sent[z, x]
+
+        @pl.when(core == 1)
+        def _():
+            place_terms(rows, weights, sent, ring_rows)
+            send(sem + 1, lambda to: sent.at[:, to % X_SIZE], along_x.at[x], x_peer, 0, X_SIZE - 1)
+            along_x[x] = sent[:, x]
+
+        meanwhile()
+
+        @pl.when(core == 0)
+        def _():
+            bytes_of(sem, landed, heads - 1).wait_recv()
+            result[...] = summed(landed, heads)
+
+        @pl.when(core == 1)
+        def _():
+            bytes_of(sem + 1, along_x, X_SIZE - 1).wait_recv()
+            part = summed(along_x, X_SIZE).astype(BF16)
+            along_z_sent[...] = part
+            send(
+                sem + 2, lambda to: along_z_sent.at[to // X_SIZE], along_z.at[z], z_peer, 0, Z_SIZE - 1
+            )
+            along_z[z] = along_z_sent[z]
+            bytes_of(sem + 1, along_x, X_SIZE - 1).wait_send()
+            bytes_of(sem + 2, along_z, Z_SIZE - 1).wait_recv()
+            result[...] = summed(along_z, Z_SIZE)
+            bytes_of(sem + 2, along_z, Z_SIZE - 1).wait_send()
+
+    def scatter_direct(sem, rows, weights, sent, landed, result, meanwhile):
+        for half in (ring_rows[:4], ring_rows[4:]):
+            place_terms(rows, weights, sent, half)
+            for offset in farthest_first(half):
+                send_to(
+                    offset,
+                    sem,
+                    lambda to: sent.at[to // X_SIZE, to % X_SIZE],
+                    landed.at[me],
+                )
+        landed[me] = sent[z, x]
+        meanwhile()
+        bytes_of(sem, landed, heads - 1).wait_recv()
+        result[...] = summed(landed, heads)
+
+    def row_factor(squares):
         mean = jnp.sum(squares, axis=1, keepdims=True) * (1.0 / (heads * width))
-        factor = lax.rsqrt(mean + EPS)
-        return jnp.concatenate(
-            [(wide[h] * factor * gains[h : h + 1, :]).astype(BF16) for h in range(heads)], axis=1
-        )
+        return lax.rsqrt(mean + EPS)
 
     def summed(blocks, count):
         total = blocks[0].astype(F32)
@@ -200,7 +319,8 @@
 
     wait_all(load_hidden)
     pl.semaphore_wait(barrier, heads - 1)
-    send(0, lambda to: hidden, gathered.at[me], any_peer, heads - 1)
+    with jax.named_scope("send_rows"):
+        gather(0, hidden, gathered.at[me])
     wait_all(load_qkv)
     wait_all(load_cache)
 
@@ -219,142 +339,189 @@
         jnp.sum(jnp.where(live, terms[...], 0.0), axis=0, keepdims=True)
     )
 
-    bytes_of(0, gathered, heads - 1).wait_recv()
-
-    normed = normed_rows(gathered, gain_one)
-    qkv = jnp.dot(normed, w_qkv[...], preferred_element_type=F32).astype(BF16)
-    query = qkv[:, 0:width]
-    new_key = qkv[:, width : 2 * width]
-    new_value = qkv[:, 2 * width : 3 * width]
-    kv_out[0] = new_key
-    kv_out[1] = new_value
-    inv_root = 1.0 / math.sqrt(width)
-    context = keys.shape[0] // samples
-    products = lax.dot_general(
-        query, keys[...], (((1,), (1,)), ((), ())), preferred_element_type=F32
-    )
-    scores = products[:, 0:context]
-    for b in range(1, samples):
-        scores = jnp.where(row == b, products[:, b * context : (b + 1) * context], scores)
-    scores = jnp.where(lane.astype(F32) < length, scores * inv_root, -jnp.inf)
-    own = (
-        jnp.sum(query.astype(F32) * new_key.astype(F32), axis=1, keepdims=True) * inv_root
-    )
-    top = jnp.maximum(jnp.max(scores, axis=1, keepdims=True), own)
-    weights = jnp.exp(scores - top)
-    own_weight = jnp.exp(own - top)
-    total = jnp.sum(weights, axis=1, keepdims=True) + own_weight
-    weights = weights / total
-    own_weight = (own_weight / total).astype(BF16).astype(F32)
-    placed = jnp.concatenate(
-        [jnp.where(row == b, weights, 0.0).astype(BF16) for b in range(samples)], axis=1
-    )
-    blended = jnp.dot(placed, values[...], preferred_element_type=F32)
-    attended = (blended + own_weight * new_value.astype(F32)).astype(BF16)
-
-    head_terms = jnp.dot(attended, w_out[...], preferred_element_type=F32).astype(BF16)
-    for h in range(heads):
-        send_heads[h] = head_terms[:, h * width : (h + 1) * width]
-    send(1, lambda to: send_heads.at[to], got_heads.at[me], any_peer, heads - 1)
-    got_heads[me] = send_heads[me]
-    wait_all(load_in)
-    filter_sum = tap_bias[...] + filters[0] * taps[0:1, :]
+    with jax.named_scope("turn_keys"):
+        keys_turned[...] = jnp.transpose(keys[...])
+
+    with jax.named_scope("rows"):
+        squares, product = projected_rows(0, gathered, gain_one, lambda at: w_qkv[at, :])
+    with jax.named_scope("attend"):
+        qkv = (product * row_factor(squares)).astype(BF16)
+        query = qkv[:, 0:width]
+        new_key = qkv[:, width : 2 * width]
+        new_value = qkv[:, 2 * width : 3 * width]
+    with jax.named_scope("scores"):
+        inv_root = 1.0 / math.sqrt(width)
+        context = keys.shape[0] // samples
+        products = jnp.dot(query, keys_turned[...], preferred_element_type=F32)
+        scores = products[:, 0:context]
+        for b in range(1, samples):
+            scores = jnp.where(row == b, products[:, b * context : (b + 1) * context], scores)
+    with jax.named_scope("softmax"):
+        scores = jnp.where(lane.astype(F32) < length, scores * inv_root, -jnp.inf)
+        own = (
+            jnp.sum(query.astype(F32) * new_key.astype(F32), axis=1, keepdims=True) * inv_root
+        )
+        top = jnp.maximum(jnp.max(scores, axis=1, keepdims=True), own)
+        weights = jnp.exp(scores - top)
+        own_weight = jnp.exp(own - top)
+        total = jnp.sum(weights, axis=1, keepdims=True) + own_weight
+        inverse = 1.0 / total
+    with jax.named_scope("blend"):
+        placed = jnp.concatenate(
+            [jnp.where(row == b, weights, 0.0).astype(BF16) for b in range(samples)], axis=1
+        )
+        blended = jnp.dot(placed, values[...], preferred_element_type=F32)
+        attended = ((blended + own_weight * new_value.astype(F32)) * inverse).astype(BF16)
+
     n_taps = taps.shape[0]
-    for k in range(1, n_taps - 1):
-        filter_sum = filter_sum + filters[k] * taps[k : k + 1, :]
-    bytes_of(1, got_heads, heads - 1).wait_recv()
-    mixed_block = (hidden[...].astype(F32) + summed(got_heads, heads)).astype(BF16)
-    mixed[...] = mixed_block
-
+
+    def while_heads_travel():
+        kv_out[0] = new_key
+        kv_out[1] = new_value
+        wait_all(load_in)
+        filter_sum = tap_bias[...] + filters[0] * taps[0:1, :]
+        for k in range(1, n_taps - 1):
+            filter_sum = filter_sum + filters[k] * taps[k : k + 1, :]
+        filtered[...] = filter_sum
+
+    with jax.named_scope("head_terms"):
+        scatter_direct(
+            8, attended, w_out, send_heads, got_heads, arrived, while_heads_travel
+        )
+    with jax.named_scope("sum_heads"):
+        mixed_block = (hidden[...].astype(F32) + arrived[...]).astype(BF16)
+        mixed[...] = mixed_block
+
+    with jax.named_scope("send_mixed"):
+        gather(9, mixed, gathered_two.at[me])
     gathered_two[me] = mixed_block
-    send(2, lambda to: mixed, gathered_two.at[me], any_peer, heads - 1)
     wait_all(load_scan)
     decay = jnp.exp(rate[...])
-    bytes_of(2, gathered_two, heads - 1).wait_recv()
-
-    normed_two = normed_rows(gathered_two, gain_two)
-    x_inner = jnp.dot(normed_two, w_in[0], preferred_element_type=F32)
-    conv_sum = filter_sum + x_inner * taps[n_taps - 1 : n_taps, :]
-    conv_out = (conv_sum * jax.nn.sigmoid(conv_sum)).astype(BF16)
-    across = (((1,), (1,)), ((), ()))
-    select_low = lax.dot_general(
-        conv_out, w_select[0:rank, :], across, preferred_element_type=F32
-    )
-    select_maps = lax.dot_general(
-        conv_out, w_select[rank:, :], across, preferred_element_type=F32
-    )
-    n_maps = 2 * n_state
-    half = width // 2
-
-    def with_rest(block):
-        high = block.astype(BF16)
-        rest = block - high.astype(F32)
-        return (high.astype(F32) + pltpu.roll(rest, half, 1)).astype(BF16)
-
-    extra = jnp.concatenate(
-        [select_maps, reward_part, jnp.zeros((samples, width - n_maps - 1), F32)], axis=1
-    )
-    packed = jnp.concatenate([select_low.astype(BF16), with_rest(extra)], axis=1)
-    send_x[...] = packed
+    with jax.named_scope("mixed_rows"):
+        squares, product = projected_rows(9, gathered_two, gain_two, lambda at: w_in[0, at, :])
+        factor_two = row_factor(squares)
+        x_inner = product * factor_two
+    with jax.named_scope("select"):
+        conv_sum = filtered[...] + x_inner * taps[n_taps - 1 : n_taps, :]
+        conv_out = (conv_sum * jax.nn.sigmoid(conv_sum)).astype(BF16)
+        selected = lax.dot_general(
+            conv_out, w_select[...], (((1,), (1,)), ((), ())), preferred_element_type=F32
+        )
+        n_maps = 2 * n_state
+        group = 8
+        stride = n_maps + group
+        at_lane = lax.broadcasted_iota(jnp.int32, (group, width), 1)
+        high_place = (at_lane == n_maps) | (at_lane == n_maps + stride) | (
+            at_lane == n_maps + 2 * stride
+        )
+        low_place = (at_lane == n_maps + 1) | (at_lane == n_maps + 1 + stride) | (
+            at_lane == n_maps + 1 + 2 * stride
+        )
+
+        def payload(low, extra):
+            rounded = extra.astype(BF16).astype(F32)
+            rest = pltpu.roll(extra - rounded, 1, 1)
+            extra = jnp.where(low_place, rest, extra)
+            return jnp.concatenate(
+                [low[:, 0:width], low[:, width : 2 * width], extra], axis=0
+            ).astype(BF16)
+
+        def opened(total):
+            low = jnp.concatenate([total[0:samples], total[samples : 2 * samples]], axis=1)
+            extra = total[2 * samples :]
+            extra = jnp.where(high_place, extra + pltpu.roll(extra, width - 1, 1), extra)
+            return low, extra
+
+        wide = jnp.concatenate(
+            [selected[:, rank:], reward_part, jnp.zeros((samples, width - n_maps - 1), F32)],
+            axis=1,
+        )
+        extra = (
+            wide[0:group]
+            + pltpu.roll(wide[group : 2 * group], stride, 1)
+            + pltpu.roll(wide[2 * group : 3 * group], 2 * stride, 1)
+        )
+        packed = payload(selected[:, 0:rank], extra)
+        send_x[...] = packed
+    with jax.named_scope("send_x"):
+        send(17, lambda to: send_x, got_x.at[x], x_peer, 0, X_SIZE - 1)
     got_x[x] = packed
-    send(3, lambda to: send_x, got_x.at[x], x_peer, X_SIZE - 1)
-    gate_part = jnp.dot(normed_two, w_in[1], preferred_element_type=F32)
-    gate = gate_part * jax.nn.sigmoid(gate_part)
-    bytes_of(3, got_x, X_SIZE - 1).wait_recv()
-
-    def joined(total):
-        low = total[:, 0:rank]
-        rest = total[:, rank:]
-        return low, jnp.where(lane < half, rest + pltpu.roll(rest, half, 1), 0.0)
-
-    low, extra = joined(summed(got_x, X_SIZE))
-    packed = jnp.concatenate([low.astype(BF16), with_rest(extra)], axis=1)
-    send_z[...] = packed
+    with jax.named_scope("gate"):
+        gate_parts = jnp.zeros((samples, channels), F32)
+        for dz in ring_rows:
+            first = row_start(dz)
+            _, scaled = scaled_row(first, gathered_two, gain_two)
+            gate_parts = gate_parts + jnp.dot(
+                scaled, w_in[1, row_at(first), :], preferred_element_type=F32
+            )
+        gate_part = gate_parts * factor_two
+        gate = gate_part * jax.nn.sigmoid(gate_part)
+    with jax.named_scope("wait_x"):
+        bytes_of(17, got_x, X_SIZE - 1).wait_recv()
+    with jax.named_scope("sum_x"):
+        low, extra = opened(summed(got_x, X_SIZE))
+        packed = payload(low, extra)
+        send_z[...] = packed
+    with jax.named_scope("send_z"):
+        send(18, lambda to: send_z, got_z.at[z], z_peer, 0, Z_SIZE - 1)
     got_z[z] = packed
-    send(4, lambda to: send_z, got_z.at[z], z_peer, Z_SIZE - 1)
     for k in range(n_taps - 2):
         filter_out[k] = filters[k + 1]
     filter_out[n_taps - 2] = x_inner
     conv_value = conv_out.astype(F32)
     skipped = skip[...] * conv_value
-    bytes_of(4, got_z, Z_SIZE - 1).wait_recv()
-    low, extra = joined(summed(got_z, Z_SIZE))
-
-    pre_step = jnp.dot(low.astype(BF16), w_step[...], preferred_element_type=F32) + step_bias[...]
-    step_size = jnp.maximum(pre_step, 0.0) + jnp.log1p(jnp.exp(-jnp.abs(pre_step)))
-    driven = step_size * conv_value
-    turned = jnp.transpose(
-        jnp.concatenate([extra, jnp.zeros((width - samples, width), F32)], axis=0)
-    )
-    rewards_out[...] = turned[n_maps : n_maps + 1, 0:samples]
-    scanned = []
-    for b in range(samples):
-        new_state = (
-            jnp.exp(-step_size[b : b + 1, :] * decay) * state[b]
-            + turned[0:n_state, b : b + 1] * driven[b : b + 1, :]
-        )
-        state_out[b] = new_state
-        scanned.append(
-            jnp.sum(turned[n_state:n_maps, b : b + 1] * new_state, axis=0, keepdims=True)
-        )
-    scan_out = ((jnp.concatenate(scanned, axis=0) + skipped) * gate).astype(BF16)
-
-    channel_terms = jnp.dot(scan_out, w_mamba[...], preferred_element_type=F32).astype(BF16)
-    for h in range(heads):
-        send_channels[h] = channel_terms[:, h * width : (h + 1) * width]
-    send(5, lambda to: send_channels.at[to], got_channels.at[me], any_peer, heads - 1)
-    got_channels[me] = send_channels[me]
-    for phase, buffer, count in (
-        (0, gathered, heads - 1),
-        (1, got_heads, heads - 1),
-        (2, gathered_two, heads - 1),
-        (3, got_x, X_SIZE - 1),
-        (4, got_z, Z_SIZE - 1),
-    ):
-        bytes_of(phase, buffer, count).wait_send()
-    bytes_of(5, got_channels, heads - 1).wait_recv()
-    hidden_out[...] = (mixed[...].astype(F32) + summed(got_channels, heads)).astype(BF16)
-    bytes_of(5, got_channels, heads - 1).wait_send()
+    with jax.named_scope("wait_z"):
+        bytes_of(18, got_z, Z_SIZE - 1).wait_recv()
+
+    with jax.named_scope("step_size"):
+        low, extra = opened(summed(got_z, Z_SIZE))
+        pre_step = (
+            jnp.dot(low.astype(BF16), w_step[...], preferred_element_type=F32) + step_bias[...]
+        )
+        step_size = jnp.maximum(pre_step, 0.0) + jnp.log1p(jnp.exp(-jnp.abs(pre_step)))
+        driven = step_size * conv_value
+        turned = jnp.transpose(
+            jnp.concatenate([extra, jnp.zeros((width - group, width), F32)], axis=0)
+        )
+    with jax.named_scope("scan"):
+        scanned = []
+        for b in range(samples):
+            base, column = (b // group) * stride, b % group
+            into = turned[base : base + n_state, column : column + 1]
+            out_of = turned[base + n_state : base + n_maps, column : column + 1]
+            new_state = (
+                jnp.exp(-step_size[b : b + 1, :] * decay) * state[b]
+                + into * driven[b : b + 1, :]
+            )
+            state_out[b] = new_state
+            scanned.append(jnp.sum(out_of * new_state, axis=0, keepdims=True))
+        scan_out = ((jnp.concatenate(scanned, axis=0) + skipped) * gate).astype(BF16)
+
+
+    def while_channels_travel():
+        rewards_out[...] = jnp.concatenate(
+            [
+                turned[k * stride + n_maps : k * stride + n_maps + 1, 0:group]
+                for k in range(samples // group)
+            ],
+            axis=1,
+        )
+        for dz in ring_rows:
+            bytes_of(dz, gathered, in_row(dz)).wait_send()
+            bytes_of(9 + dz, gathered_two, in_row(dz)).wait_send()
+        bytes_of(8, got_heads, heads - 1).wait_send()
+        bytes_of(17, got_x, X_SIZE - 1).wait_send()
+        bytes_of(18, got_z, Z_SIZE - 1).wait_send()
+
+    with jax.named_scope("channel_terms"):
+        scatter_sums(
+            19, scan_out, w_mamba, send_channels, got_channels, arrived, while_channels_travel
+        )
+    hidden_out[...] = (mixed[...].astype(F32) + arrived[...]).astype(BF16)
+
+    @pl.when(core == 0)
+    def _():
+        bytes_of(19, got_channels, heads - 1).wait_send()
 
 
 def write_kernel(*refs):
@@ -401,7 +568,7 @@
     select = w_select.shape[1]
     n_taps = filter_weight.shape[0]
     n_state = log_rate.shape[0]
-    lanes = -(-select // width) * width
+    packed = 2 * samples + 8
     operands = (
         hidden_in,
         attention_gain.reshape(heads, width),
@@ -431,6 +598,7 @@
         pltpu.VMEM((features, 3 * width), BF16),
         pltpu.VMEM((width, features), BF16),
         pltpu.VMEM((samples * context, head_size), BF16),
+        pltpu.VMEM((head_size, samples * context), BF16),
         pltpu.VMEM((samples * context, head_size), BF16),
         pltpu.VMEM((1, samples), jnp.int32),
         pltpu.VMEM((heads, width), F32),
@@ -448,19 +616,24 @@
         pltpu.VMEM(reward_terms.shape[::-1], F32),
         pltpu.VMEM(reward_mask.shape[::-1], jnp.int32),
         pltpu.VMEM((heads, samples, width), BF16),
-        pltpu.VMEM((heads, samples, width), BF16),
+        pltpu.VMEM((Z_SIZE, X_SIZE, samples, width), BF16),
         pltpu.VMEM((heads, samples, width), BF16),
         pltpu.VMEM((samples, width), BF16),
         pltpu.VMEM((heads, samples, width), BF16),
-        pltpu.VMEM((samples, lanes), BF16),
-        pltpu.VMEM((X_SIZE, samples, lanes), BF16),
-        pltpu.VMEM((samples, lanes), BF16),
-        pltpu.VMEM((Z_SIZE, samples, lanes), BF16),
-        pltpu.VMEM((heads, samples, width), BF16),
+        pltpu.VMEM((packed, width), BF16),
+        pltpu.VMEM((X_SIZE, packed, width), BF16),
+        pltpu.VMEM((packed, width), BF16),
+        pltpu.VMEM((Z_SIZE, packed, width), BF16),
+        pltpu.VMEM((Z_SIZE, X_SIZE, samples, width), BF16),
         pltpu.VMEM((heads, samples, width), BF16),
         pltpu.SemaphoreType.DMA((24,)),
-        pltpu.SemaphoreType.DMA((6,)),
-        pltpu.SemaphoreType.DMA((6,)),
+        pltpu.VMEM((samples, channels), F32),
+        pltpu.VMEM((samples, width), F32),
+        pltpu.VMEM((X_SIZE, Z_SIZE, samples, width), BF16),
+        pltpu.VMEM((Z_SIZE, samples, width), BF16),
+        pltpu.VMEM((Z_SIZE, samples, width), BF16),
+        pltpu.SemaphoreType.DMA((27,)),
+        pltpu.SemaphoreType.DMA((27,)),
     ]
     vmem = pl.BlockSpec(memory_space=pltpu.VMEM)
     hbm = pl.BlockSpec(memory_space=pltpu.HBM)

time: 51.1 us -> 49.3 us (0.965)
  Pallas kernels: 50.3 us -> 48.5 us
    pallas_call x1, Pallas kernels: 49.4 us -> 47.7 us  [local(): pl.pallas_call(step_kernel, out_shape=tuple((pltpu.VMEM(shape, dtype) for...]
where the time goes in v2:
time: 49.3 us; the launch traced here: 49.1 us
  Pallas kernels  48.5 us (98%)
  between operations  0.65 us (1%)
    pallas_call x1, Pallas kernels, local(): pl.pallas_call(step_kernel, out_shape=tuple((pltpu.VMEM(shape, dtype) for...  47.7 us

profile of v2, /device:TPU:8, one launch (start us, length us, event | category | flops | bytes accessed | tf_op | source)
XLA Modules:
  0.0 49.1 jit_solution(6418866799525017870)
XLA Ops:
  0.6 47.7 %decode_step.1 = (bf16[24,128]{1,0:T(8,128)(2,1)S(1)}, bf16[2,24,128]{2,1,0:T(8,128)(2,1)S(1)}, f32[3,24,256]{2,1,0:T(8,128)S(1)}, f32[24,16,256]{2,1,0:T(8,128)S(1)}, f32[1,24]{1,0:T(1,128)S(1)}) custom-call(bf16[24,128]{1,0:T(8,128)(2,1)} %hidden_hbm.1, f32[32,128]{1,0:T(8,128)} %bitcast.19, bf16[4096,128]{1,0:T(8,128)(2,1)} %w_query_hbm.1, ...), custom_call_target="tpu_custom_call" | custom-call | tf_op jit(solution)/shard_map/decode_step/pallas_call | solution.py:647
  48.3 0.8 %write_results.1 = (bf16[24,128]{1,0:T(8,128)(2,1)}, bf16[2,24,128]{2,1,0:T(8,128)(2,1)}, f32[3,24,256]{2,1,0:T(8,128)}, f32[24,16,256]{2,1,0:T(8,128)}, f32[1,24]{1,0:T(1,128)}) custom-call(bf16[24,128]{1,0:T(8,128)(2,1)S(1)} %get-tuple-element.15.refs_0_, bf16[2,24,128]{2,1,0:T(8,128)(2,1)S(1)} %get-tuple-element.16.refs_1_, ...), custom_call_target="tpu_custom_call" | custom-call | tf_op jit(solution)/shard_map/write_results/pallas_call | solution.py:658
